TPU v7x, 128 devices: a whole 4x4x4 slice. The times are simulated.
128 devices in a mesh: dp: 16 (over z, x), expert: 8 (over y, core).
Axes of the slice: x: 4, y: 4, z: 4, core: 2. Of those that a mesh axis runs over, the one named last changes fastest.
Arguments:
- tokens: bfloat16 [16384, 2048], P(('dp', 'expert')), may hold values from -6 to 6
- cotangent: bfloat16 [16384, 2048], P(('dp', 'expert')), may hold values from -6 to 6
- expert_ids: int32 [16384, 2], P(('dp', 'expert')), may hold values from 0 to 7, all different within a row; in each aligned block of 128 rows (0 to 127, 128 to 255, ...) at most 36 rows name the same one
- route_share: float32 [16384], P(('dp', 'expert')), may hold values from 0.5 to 0.95
- gate_proj: bfloat16 [8, 7168, 2048], P('expert', 'dp'), may hold values from -0.125 to 0.125
- up_proj: bfloat16 [8, 7168, 2048], P('expert', 'dp'), may hold values from -0.125 to 0.125
- down_anchor: float32 [8, 7168, 2048], P('expert', 'dp'), may hold values from -0.12 to 0.12
- down_average: float32 [8, 7168, 2048], P('expert', 'dp'), may hold values from -0.12 to 0.12
- down_moment: float32 [8, 7168, 2048], P('expert', 'dp'), may hold values from 0.002 to 0.05
Outputs:
- new_anchor: float32 [8, 7168, 2048], P('expert', 'dp')
- new_average: float32 [8, 7168, 2048], P('expert', 'dp')
- new_moment: float32 [8, 7168, 2048], P('expert', 'dp')
Inputs may be any that keep to these rules, and one draw needn't show every extreme that they name: `expert_ids`: the two ids of a token differ. The rows of one device name any expert at most 36 times, and in every draw some device names some expert exactly 36 times.
All inputs are finite; a program needn't handle non-finite values.
Results may differ from a plain program's by a relative error of at most 0.0043.
Values may be sent and summed in bfloat16 or wider, within the bound.
No kernel may reach another device: no remote copies, remote signals or barrier semaphores. Data moves between devices by JAX's collectives and lax.ppermute only.
A program may use at most 192 MiB of HBM per device.

v0:
```python
import jax
import jax.numpy as jnp
from jax import lax
from jax.sharding import PartitionSpec as P

FF = 7168
TOPK = 2
beta_one = 0.9
beta_two = 0.95
learn_rate = 0.05
decay_rate = 0.1
step_count = 4.0
epsilon = 1e-08


def expert_terms(pieces, weight_gate, weight_up):
    rows_in, gated_rows = pieces
    gate_act = lax.dot_general(
        rows_in, weight_gate, (((1,), (1,)), ((), ())), preferred_element_type=jnp.float32
    )
    up_act = lax.dot_general(
        rows_in, weight_up, (((1,), (1,)), ((), ())), preferred_element_type=jnp.float32
    )
    hidden = (jax.nn.silu(gate_act) * up_act).astype(jnp.bfloat16)
    return lax.dot_general(
        hidden, gated_rows, (((0,), (0,)), ((), ())), preferred_element_type=jnp.float32
    )


def shards(
    tokens,
    cotangent,
    expert_ids,
    route_share,
    gate_proj,
    up_proj,
    down_anchor,
    down_average,
    down_moment,
):
    experts_all = lax.axis_size("expert")
    tok_rows = tokens.shape[0]
    width = tokens.shape[1]
    capacity = tok_rows * TOPK // experts_all * 9 // 8
    slots = experts_all * capacity
    shares = jnp.stack([route_share, 1.0 - route_share], axis=1)
    expert_range = jnp.arange(experts_all, dtype=jnp.int32)
    flat_ids = expert_ids.reshape(-1)
    onehot_routes = (flat_ids[:, None] == expert_range[None, :]).astype(jnp.int32)
    earlier = jnp.cumsum(onehot_routes, axis=0) - onehot_routes
    slot_of = jnp.sum(earlier * onehot_routes, axis=1)
    target = (flat_ids * capacity + slot_of).reshape(tok_rows, TOPK)
    slot_range = jnp.arange(slots, dtype=jnp.int32)
    placed = target[None, :, :] == slot_range[:, None, None]
    picker = jnp.sum(placed.astype(jnp.float32), axis=2).astype(jnp.bfloat16)
    slot_share = jnp.sum(jnp.where(placed, shares[None, :, :], 0.0), axis=(1, 2))
    send_rows = jnp.dot(picker, tokens, preferred_element_type=jnp.float32).astype(jnp.bfloat16)
    send_grad = (
        slot_share[:, None] * jnp.dot(picker, cotangent, preferred_element_type=jnp.float32)
    ).astype(jnp.bfloat16)
    weight_gate = gate_proj[0]
    weight_up = up_proj[0]
    arrived = (
        lax.all_to_all(
            send_rows.reshape(experts_all, capacity, width),
            "expert",
            split_axis=0,
            concat_axis=0,
            tiled=True,
        ),
        lax.all_to_all(
            send_grad.reshape(experts_all, capacity, width),
            "expert",
            split_axis=0,
            concat_axis=0,
            tiled=True,
        ),
    )
    rows_here = arrived[0].reshape(slots, width)
    grad_here = arrived[1].reshape(slots, width)
    gradient = expert_terms(
        (
            lax.all_gather(rows_here, "dp", axis=0, tiled=True),
            lax.all_gather(grad_here, "dp", axis=0, tiled=True),
        ),
        weight_gate,
        weight_up,
    )
    gradient = gradient[None] * FF ** (-0.5)
    bias_two = 1.0 - beta_two**step_count
    eval_point = (1.0 - beta_one) * down_anchor + beta_one * down_average
    second_moment = beta_two * down_moment + (1.0 - beta_two) * gradient * gradient
    update_dir = gradient / (jnp.sqrt(second_moment / bias_two) + epsilon) + decay_rate * eval_point
    new_anchor = down_anchor - learn_rate * update_dir
    new_average = (1.0 - 1.0 / step_count) * down_average + 1.0 / step_count * new_anchor
    return (new_anchor, new_average, second_moment)


def solution(mesh):
    placed = (
        P(("dp", "expert"), None),
        P(("dp", "expert"), None),
        P(("dp", "expert"), None),
        P(("dp", "expert")),
        P("expert", "dp", None),
        P("expert", "dp", None),
        P("expert", "dp", None),
        P("expert", "dp", None),
        P("expert", "dp", None),
    )
    return jax.shard_map(
        shards,
        mesh=mesh,
        in_specs=placed,
        out_specs=(P("expert", "dp", None), P("expert", "dp", None), P("expert", "dp", None)),
        check_vma=False,
    )
```

profile of v0, /device:TPU:1, one launch (start us, length us, event | category | flops | bytes accessed | tf_op | source)
XLA Modules:
  0.0 330.5 jit_solution(17586150212628106540)
XLA Ops:
  7.2 0.0 copy-start
  7.2 0.0 all-gather.3.cloned.1.call-start
  7.2 0.9 copy.24
  8.1 0.1 eq.42
  8.3 0.1 eq.38
  8.4 0.7 subtract_bitcast_fusion
  9.1 0.6 reduce-window.6
  9.7 0.2 slice_reduce_fusion
  9.9 0.1 fusion.11
  10.0 0.1 reduce_sum.30
  10.2 0.1 copy.26
  10.2 0.7 multiply_add_fusion.1
  10.9 0.7 pad_maximum_fusion
  11.6 0.2 select_reduce_fusion
  11.7 2.5 convolution_convert_fusion
  14.2 1.4 reshape.48
  15.6 23.6 %all_to_all.10 = bf16[8,36,2048]{2,1,0:T(8,128)(2,1)} all-to-all(bf16[8,36,2048]{2,1,0:T(8,128)(2,1)S(1)} %reshape.48), channel_id=1, replica_groups=mesh['dp'=16,'expert'=8] {'expert'}, dimensions={0} | all-to-all | bytes 2359296 | tf_op jit(solution)/shard_map/all_to_all | solution.py:64
  39.2 0.0 copy-start.1
  39.2 2.3 reshape.49
  41.5 0.0 all-gather.3.cloned.1.call-update
  41.5 0.0 all-gather.5.cloned.1.call-start
  41.6 0.0 copy-done.1
  41.6 1.5 fusion.4
  43.1 1.4 reshape.50
  44.5 21.9 %all_to_all.11 = bf16[8,36,2048]{2,1,0:T(8,128)(2,1)} all-to-all(bf16[8,36,2048]{2,1,0:T(8,128)(2,1)S(1)} %reshape.50), channel_id=1, replica_groups=mesh['dp'=16,'expert'=8] {'expert'}, dimensions={0} | all-to-all | bytes 2359296 | tf_op jit(solution)/shard_map/all_to_all | solution.py:71
  66.4 2.2 reshape.51
  68.6 0.0 all-gather.5.cloned.1.call-update
  68.6 95.7 %all-gather.3.cloned.1.call-done = bf16[4608,2048]{1,0:T(8,128)(2,1)} async-done(((bf16[288,2048]{1,0:T(8,128)(2,1)}), bf16[4608,2048]{1,0:T(8,128)(2,1)}) %all-gather.3.cloned.1.call-update) | async-done | bytes 18874384 | tf_op jit(solution)/shard_map/all_gather | solution.py:83
  164.3 15.2 %fusion.6 = f32[4608,448]{0,1:T(8,128)} fusion(bf16[4608,2048]{1,0:T(8,128)(2,1)} %all-gather.3.cloned.1.call-done, bf16[1,448,2048]{2,1,0:T(8,128)(2,1)} %param.13), kind=kOutput, calls=%fused_computation.12 | convolution fusion | flops 8455716864 | bytes 28966912 | tf_op jit(solution)/shard_map/dot_general | solution.py:18
  179.5 109.2 %all-gather.5.cloned.1.call-done = bf16[4608,2048]{1,0:T(8,128)(2,1)} async-done(((bf16[288,2048]{1,0:T(8,128)(2,1)}), bf16[4608,2048]{1,0:T(8,128)(2,1)}) %all-gather.5.cloned.1.call-update) | async-done | bytes 18874384 | tf_op jit(solution)/shard_map/all_gather | solution.py:84
  288.7 0.0 copy-done
  288.7 34.9 %multiply_add_fusion = (f32[1,448,2048]{2,1,0:T(8,128)}, f32[1,448,2048]{2,1,0:T(8,128)}, f32[1,448,2048]{2,1,0:T(8,128)}) fusion(f32[1,448,2048]{2,1,0:T(8,128)} %param.16, f32[1,448,2048]{2,1,0:T(8,128)} %param.15, f32[1,448,2048]{2,1,0:T(8,128)} %param.17, bf16[4608,2048]{1,0:T(8,128)(2,1)} %all-gather.5.cloned.1.call-done, ...), kind=kOutput, calls=%fused_computation.7 | convolution fusion | flops 16940335104 | bytes 69861376 | tf_op jit(solution)/shard_map/dot_general | solution.py:25
  (3 shorter events, 0.0 us)
Async XLA Ops:
  7.2 281.5 %copy-start = (bf16[1,448,2048]{2,1,0:T(8,128)(2,1)S(1)}, bf16[1,448,2048]{2,1,0:T(8,128)(2,1)}, u32[]{:S(2)}) copy-start(bf16[1,448,2048]{2,1,0:T(8,128)(2,1)} %param.14) | copy-start | bytes 5505028
  7.2 157.1 %all-gather.3.cloned.1.call-start = ((), (), s32[]{:S(2)}) async-start(), calls=%async_computation.2 | async-start | bytes 20054016 | tf_op jit(solution)/shard_map/all_gather | solution.py:83
  39.2 2.4 copy-start.1
  41.5 247.1 %all-gather.5.cloned.1.call-start = ((), (), s32[]{:S(2)}) async-start(), calls=%async_computation.3 | async-start | bytes 20054016 | tf_op jit(solution)/shard_map/all_gather | solution.py:84
Sparse Core Ops, SparseCore 0:
  41.7 122.6 all-gather.2
  167.0 121.6 all-gather.4
where the time goes:
time: 331 us; the launch traced here: 330 us
  waiting for transfers between devices  205 us (62%)
  matrix products  54.1 us (16%)
  blocking collectives  45.5 us (14%)
  between operations  14.1 us (4%)
  local copies, waits for them, and re-layouts  8.88 us (3%)
    all_gather x1, waiting for transfers between devices, shards(): lax.all_gather(grad_here, 'dp', axis=0, tiled=True)  109 us
    all_gather x1, waiting for transfers between devices, shards(): lax.all_gather(rows_here, 'dp', axis=0, tiled=True)  95.7 us
    dot_general x1, matrix products, expert_terms(): lax.dot_general(hidden, gated_rows, (((0,), (0,)), ((), ())), preferred_e...  34.9 us
    all_to_all x1, blocking collectives, shards(): lax.all_to_all(send_rows.reshape(experts_all, capacity, width), 'expert',...  23.6 us
    all_to_all x1, blocking collectives, shards(): lax.all_to_all(send_grad.reshape(experts_all, capacity, width), 'expert',...  21.9 us
    dot_general x1, matrix products, expert_terms(): lax.dot_general(rows_in, weight_gate, (((1,), (1,)), ((), ())), preferred...  15.2 us
  transfers between devices with their start and end apart: 2, of which 2 were waited for; matrix products, arithmetic and copies ran while one was open for 6% of the time, Pallas kernels for 0%

commit v1 on v0

--- a/solution.py
+++ b/solution.py
@@ -11,6 +11,19 @@
 decay_rate = 0.1
 step_count = 4.0
 epsilon = 1e-08
+
+
+def ring_gather(shard, axis, dim):
+    ways = lax.axis_size(axis)
+    up = [(d, (d + 1) % ways) for d in range(ways)]
+    down = [(d, (d - 1) % ways) for d in range(ways)]
+    earlier, later = ([shard], [shard])
+    for _ in range(ways // 2):
+        earlier.append(lax.ppermute(earlier[-1], axis, up))
+    for _ in range((ways - 1) // 2):
+        later.append(lax.ppermute(later[-1], axis, down))
+    line = jnp.concatenate([*earlier[::-1], *later[1:]], axis=dim)
+    return jnp.roll(line, (lax.axis_index(axis) - ways // 2) * shard.shape[dim], axis=dim)
 
 
 def expert_terms(pieces, weight_gate, weight_up):
@@ -79,10 +92,7 @@
     rows_here = arrived[0].reshape(slots, width)
     grad_here = arrived[1].reshape(slots, width)
     gradient = expert_terms(
-        (
-            lax.all_gather(rows_here, "dp", axis=0, tiled=True),
-            lax.all_gather(grad_here, "dp", axis=0, tiled=True),
-        ),
+        (lax.all_gather(rows_here, "dp", axis=0, tiled=True), ring_gather(grad_here, "dp", 0)),
         weight_gate,
         weight_up,
     )

time: 331 us -> 476 us (1.44); the launches traced: 330 us -> 467 us
  local copies, waits for them, and re-layouts: 8.88 us -> 61.7 us
  waiting for transfers between devices: 205 us -> 252 us
  starting transfers between devices: 0.08 us -> 35.7 us
    ppermute x0 -> x15, waiting for transfers between devices: none -> 252 us  [the longest x8 252 us: ring_gather(): earlier.append(lax.ppermute(earlier[-1], axis, up))]
    all_gather x1 -> x0, waiting for transfers between devices: 109 us -> none  [shards(): lax.all_gather(grad_here, 'dp', axis=0, tiled=True)]
    all_gather x1, waiting for transfers between devices: 95.7 us -> 0.01 us  [shards(): lax.all_gather(rows_here, 'dp', axis=0, tiled=True)]
    unnamed x5 -> x66, local copies, waits for them, and re-layouts: 0.92 us -> 53.4 us
    ppermute x0 -> x15, starting transfers between devices: none -> 35.7 us  [the longest x7 34.4 us: ring_gather(): later.append(lax.ppermute(later[-1], axis, down))]
  transfers between devices with their start and end apart: 2 -> 16, of which waited for: 2 -> 8; matrix products, arithmetic and copies ran while one was open for 6% -> 12% of each run, Pallas kernels for 0% -> 0%
where the time goes in v1:
time: 476 us; the launch traced here: 467 us
  waiting for transfers between devices  252 us (53%)
  local copies, waits for them, and re-layouts  61.7 us (13%)
  matrix products  55.4 us (12%)
  blocking collectives  45.5 us (10%)
  starting transfers between devices  35.7 us (8%)
  between operations  14.2 us (3%)
    ppermute x8, waiting for transfers between devices, ring_gather(): earlier.append(lax.ppermute(earlier[-1], axis, up))  252 us
    unnamed x66, local copies, waits for them, and re-layouts  53.4 us
    dot_general x1, matrix products, expert_terms(): lax.dot_general(hidden, gated_rows, (((0,), (0,)), ((), ())), preferred_e...  35.3 us
    ppermute x7, starting transfers between devices, ring_gather(): later.append(lax.ppermute(later[-1], axis, down))  34.4 us
    all_to_all x1, blocking collectives, shards(): lax.all_to_all(send_rows.reshape(experts_all, capacity, width), 'expert',...  23.6 us
    all_to_all x1, blocking collectives, shards(): lax.all_to_all(send_grad.reshape(experts_all, capacity, width), 'expert',...  21.9 us
    dot_general x1, matrix products, expert_terms(): lax.dot_general(rows_in, weight_gate, (((1,), (1,)), ((), ())), preferred...  15.1 us
  transfers between devices with their start and end apart: 16, of which 8 were waited for; matrix products, arithmetic and copies ran while one was open for 12% of the time, Pallas kernels for 0%

profile of v1, /device:TPU:1, one launch (start us, length us, event | category | flops | bytes accessed | tf_op | source)
XLA Modules:
  0.0 467.5 jit_solution(18371666901626123693)
XLA Ops:
  11.8 2.5 convolution_convert_fusion
  15.6 23.6 %all_to_all.10 = bf16[8,36,2048]{2,1,0:T(8,128)(2,1)} all-to-all(bf16[8,36,2048]{2,1,0:T(8,128)(2,1)S(1)} %reshape.48), channel_id=1, replica_groups=mesh['dp'=16,'expert'=8] {'expert'}, dimensions={0} | all-to-all | bytes 2359296 | tf_op jit(solution)/shard_map/all_to_all | solution.py:77
  41.5 2.5 fusion.6
  45.4 21.9 %all_to_all.11 = bf16[8,36,2048]{2,1,0:T(8,128)(2,1)} all-to-all(bf16[8,36,2048]{2,1,0:T(8,128)(2,1)S(1)} %reshape.50), channel_id=1, replica_groups=mesh['dp'=16,'expert'=8] {'expert'}, dimensions={0} | all-to-all | bytes 2359296 | tf_op jit(solution)/shard_map/all_to_all | solution.py:84
  70.1 43.5 %collective-permute-done = bf16[288,2048]{1,0:T(8,128)(2,1)S(1)} collective-permute-done((bf16[288,2048]{1,0:T(8,128)(2,1)S(1)}, bf16[288,2048]{1,0:T(8,128)(2,1)S(1)}, u32[]{:S(2)}, u32[]{:S(2)}) %collective-permute-start) | collective-permute-done | bytes 1179680 | tf_op jit(solution)/shard_map/ppermute | solution.py:22
  113.6 4.8 %collective-permute-start.8 = (bf16[288,2048]{1,0:T(8,128)(2,1)S(1)}, bf16[288,2048]{1,0:T(8,128)(2,1)S(1)}, u32[]{:S(2)}, u32[]{:S(2)}) collective-permute-start(bf16[288,2048]{1,0:T(8,128)(2,1)S(1)} %reshape.51), channel_id=1, source_target_pairs={{0,120},{8,0},{16,8},{24,16},{32,24},{40,32},{48,40},{56,48},{64,5... | collective-permute-start | bytes 3538952 | tf_op jit(solution)/shard_map/ppermute | solution.py:24
  118.3 51.3 %collective-permute-done.1 = bf16[288,2048]{1,0:T(8,128)(2,1)S(1)} collective-permute-done((bf16[288,2048]{1,0:T(8,128)(2,1)S(1)}, bf16[288,2048]{1,0:T(8,128)(2,1)S(1)}, u32[]{:S(2)}, u32[]{:S(2)}) %collective-permute-start.1) | collective-permute-done | bytes 1179680 | tf_op jit(solution)/shard_map/ppermute | solution.py:22
  169.7 4.8 %collective-permute-start.9 = (bf16[288,2048]{1,0:T(8,128)(2,1)S(1)}, bf16[288,2048]{1,0:T(8,128)(2,1)S(1)}, u32[]{:S(2)}, u32[]{:S(2)}) collective-permute-start(bf16[288,2048]{1,0:T(8,128)(2,1)S(1)} %collective-permute-done.8), channel_id=1, source_target_pairs={{0,120},{8,0},{16,8},{24,16},{32,24},{40,32},{48,40},{56,48},{64,5... | collective-permute-start | bytes 3538952 | tf_op jit(solution)/shard_map/ppermute | solution.py:24
  174.5 51.0 %collective-permute-done.2 = bf16[288,2048]{1,0:T(8,128)(2,1)S(1)} collective-permute-done((bf16[288,2048]{1,0:T(8,128)(2,1)S(1)}, bf16[288,2048]{1,0:T(8,128)(2,1)S(1)}, u32[]{:S(2)}, u32[]{:S(2)}) %collective-permute-start.2) | collective-permute-done | bytes 1179680 | tf_op jit(solution)/shard_map/ppermute | solution.py:22
  225.6 4.8 %collective-permute-start.10 = (bf16[288,2048]{1,0:T(8,128)(2,1)S(1)}, bf16[288,2048]{1,0:T(8,128)(2,1)S(1)}, u32[]{:S(2)}, u32[]{:S(2)}) collective-permute-start(bf16[288,2048]{1,0:T(8,128)(2,1)S(1)} %collective-permute-done.9), channel_id=1, source_target_pairs={{0,120},{8,0},{16,8},{24,16},{32,24},{40,32},{48,40},{56,48},{64,5... | collective-permute-start | bytes 3538952 | tf_op jit(solution)/shard_map/ppermute | solution.py:24
  230.4 23.0 %collective-permute-done.3 = bf16[288,2048]{1,0:T(8,128)(2,1)S(1)} collective-permute-done((bf16[288,2048]{1,0:T(8,128)(2,1)S(1)}, bf16[288,2048]{1,0:T(8,128)(2,1)S(1)}, u32[]{:S(2)}, u32[]{:S(2)}) %collective-permute-start.3) | collective-permute-done | bytes 1179680 | tf_op jit(solution)/shard_map/ppermute | solution.py:22
  253.5 4.8 %collective-permute-start.11 = (bf16[288,2048]{1,0:T(8,128)(2,1)S(1)}, bf16[288,2048]{1,0:T(8,128)(2,1)S(1)}, u32[]{:S(2)}, u32[]{:S(2)}) collective-permute-start(bf16[288,2048]{1,0:T(8,128)(2,1)S(1)} %collective-permute-done.10), channel_id=1, source_target_pairs={{0,120},{8,0},{16,8},{24,16},{32,24},{40,32},{48,40},{56,48},{64,5... | collective-permute-start | bytes 3538952 | tf_op jit(solution)/shard_map/ppermute | solution.py:24
  258.3 22.3 %collective-permute-done.4 = bf16[288,2048]{1,0:T(8,128)(2,1)} collective-permute-done((bf16[288,2048]{1,0:T(8,128)(2,1)S(1)}, bf16[288,2048]{1,0:T(8,128)(2,1)}, u32[]{:S(2)}, u32[]{:S(2)}) %collective-permute-start.4) | collective-permute-done | bytes 1179680 | tf_op jit(solution)/shard_map/ppermute | solution.py:22
  281.6 4.8 %collective-permute-start.12 = (bf16[288,2048]{1,0:T(8,128)(2,1)S(1)}, bf16[288,2048]{1,0:T(8,128)(2,1)}, u32[]{:S(2)}, u32[]{:S(2)}) collective-permute-start(bf16[288,2048]{1,0:T(8,128)(2,1)S(1)} %collective-permute-done.11), channel_id=1, source_target_pairs={{0,120},{8,0},{16,8},{24,16},{32,24},{40,32},{48,40},{56,48},{64,5... | collective-permute-start | bytes 3538952 | tf_op jit(solution)/shard_map/ppermute | solution.py:24
  286.4 20.7 %collective-permute-done.5 = bf16[288,2048]{1,0:T(8,128)(2,1)} collective-permute-done((bf16[288,2048]{1,0:T(8,128)(2,1)}, bf16[288,2048]{1,0:T(8,128)(2,1)}, u32[]{:S(2)}, u32[]{:S(2)}) %collective-permute-start.5) | collective-permute-done | bytes 1179680 | tf_op jit(solution)/shard_map/ppermute | solution.py:22
  307.1 5.3 %collective-permute-start.13 = (bf16[288,2048]{1,0:T(8,128)(2,1)}, bf16[288,2048]{1,0:T(8,128)(2,1)}, u32[]{:S(2)}, u32[]{:S(2)}) collective-permute-start(bf16[288,2048]{1,0:T(8,128)(2,1)} %collective-permute-done.12), channel_id=1, source_target_pairs={{0,120},{8,0},{16,8},{24,16},{32,24},{40,32},{48,40},{56,48},{64,5... | collective-permute-start | bytes 3538952 | tf_op jit(solution)/shard_map/ppermute | solution.py:24
  312.4 20.3 %collective-permute-done.6 = bf16[288,2048]{1,0:T(8,128)(2,1)} collective-permute-done((bf16[288,2048]{1,0:T(8,128)(2,1)}, bf16[288,2048]{1,0:T(8,128)(2,1)}, u32[]{:S(2)}, u32[]{:S(2)}) %collective-permute-start.6) | collective-permute-done | bytes 1179680 | tf_op jit(solution)/shard_map/ppermute | solution.py:22
  332.8 5.0 %collective-permute-start.14 = (bf16[288,2048]{1,0:T(8,128)(2,1)}, bf16[288,2048]{1,0:T(8,128)(2,1)S(1)}, u32[]{:S(2)}, u32[]{:S(2)}) collective-permute-start(bf16[288,2048]{1,0:T(8,128)(2,1)} %collective-permute-done.13), channel_id=1, source_target_pairs={{0,120},{8,0},{16,8},{24,16},{32,24},{40,32},{48,40},{56,48},{64,5... | collective-permute-start | bytes 3538952 | tf_op jit(solution)/shard_map/ppermute | solution.py:24
  337.8 19.8 %collective-permute-done.7 = bf16[288,2048]{1,0:T(8,128)(2,1)} collective-permute-done((bf16[288,2048]{1,0:T(8,128)(2,1)}, bf16[288,2048]{1,0:T(8,128)(2,1)}, u32[]{:S(2)}, u32[]{:S(2)}) %collective-permute-start.7) | collective-permute-done | bytes 1179680 | tf_op jit(solution)/shard_map/ppermute | solution.py:22
  357.5 2.4 constant_dynamic-update-slice_fusion.31
  362.4 2.5 constant_dynamic-update-slice_fusion.29
  364.9 2.5 constant_dynamic-update-slice_fusion.28
  377.9 2.4 constant_dynamic-update-slice_fusion.18
  380.3 2.4 constant_dynamic-update-slice_fusion.17
  383.9 2.4 constant_dynamic-update-slice_fusion.15
  386.4 2.4 constant_dynamic-update-slice_fusion.14
  388.8 2.5 constant_dynamic-update-slice_fusion.13
  391.2 2.4 constant_dynamic-update-slice_fusion.12
  404.1 2.4 constant_dynamic-update-slice_fusion.2
  406.6 2.4 constant_dynamic-update-slice_fusion.1
  410.2 15.1 %fusion.10 = f32[4608,448]{0,1:T(8,128)} fusion(bf16[4608,2048]{1,0:T(8,128)(2,1)} %all-gather.2.cloned.1.call-done, bf16[1,448,2048]{2,1,0:T(8,128)(2,1)} %param.13), kind=kOutput, calls=%fused_computation.14 | convolution fusion | flops 8455716864 | bytes 28966912 | tf_op jit(solution)/shard_map/dot_general | solution.py:31
  425.3 35.3 %multiply_add_fusion = (f32[1,448,2048]{2,1,0:T(8,128)}, f32[1,448,2048]{2,1,0:T(8,128)}, f32[1,448,2048]{2,1,0:T(8,128)}) fusion(f32[1,448,2048]{2,1,0:T(8,128)} %param.16, f32[1,448,2048]{2,1,0:T(8,128)} %param.15, f32[1,448,2048]{2,1,0:T(8,128)} %param.17, bf16[9216,2048]{1,0:T(8,128)(2,1)} %constant_dynamic-update-slice_fusion, s32[]{:T(128)S(6)} %select_n.19, ...), kind=kOutput, calls=%fused_computation.9 | convolution fusion | flops 16940335104 | bytes 69861376 | tf_op jit(solution)/shard_map/dot_general | solution.py:38
  (92 shorter events, 39.1 us)
Async XLA Ops:
  7.2 418.1 %copy-start = (bf16[1,448,2048]{2,1,0:T(8,128)(2,1)S(1)}, bf16[1,448,2048]{2,1,0:T(8,128)(2,1)}, u32[]{:S(2)}) copy-start(bf16[1,448,2048]{2,1,0:T(8,128)(2,1)} %param.14) | copy-start | bytes 5505028
  7.2 403.0 %all-gather.2.cloned.1.call-start = ((), (), s32[]{:S(2)}) async-start(), calls=%async_computation.2 | async-start | bytes 20054016 | tf_op jit(solution)/shard_map/all_gather | solution.py:95
  68.8 44.8 %collective-permute-start = (bf16[288,2048]{1,0:T(8,128)(2,1)S(1)}, bf16[288,2048]{1,0:T(8,128)(2,1)S(1)}, u32[]{:S(2)}, u32[]{:S(2)}) collective-permute-start(bf16[288,2048]{1,0:T(8,128)(2,1)S(1)} %reshape.51), channel_id=1, source_target_pairs={{0,8},{8,16},{16,24},{24,32},{32,40},{40,48},{48,56},{56,64},{64,7... | collective-permute-start | bytes 3538952 | tf_op jit(solution)/shard_map/ppermute | solution.py:22
  113.6 56.1 %copy-start.1 = (bf16[288,2048]{1,0:T(8,128)(2,1)}, bf16[288,2048]{1,0:T(8,128)(2,1)S(1)}, u32[]{:S(2)}) copy-start(bf16[288,2048]{1,0:T(8,128)(2,1)S(1)} %collective-permute-done) | copy-start | bytes 3538948
  113.6 56.1 %collective-permute-start.1 = (bf16[288,2048]{1,0:T(8,128)(2,1)S(1)}, bf16[288,2048]{1,0:T(8,128)(2,1)S(1)}, u32[]{:S(2)}, u32[]{:S(2)}) collective-permute-start(bf16[288,2048]{1,0:T(8,128)(2,1)S(1)} %collective-permute-done), channel_id=1, source_target_pairs={{0,8},{8,16},{16,24},{24,32},{32,40},{40,48},{48,56},{56,64},{64,7... | collective-permute-start | bytes 3538952 | tf_op jit(solution)/shard_map/ppermute | solution.py:22
  113.6 56.1 %collective-permute-start.8 = (bf16[288,2048]{1,0:T(8,128)(2,1)S(1)}, bf16[288,2048]{1,0:T(8,128)(2,1)S(1)}, u32[]{:S(2)}, u32[]{:S(2)}) collective-permute-start(bf16[288,2048]{1,0:T(8,128)(2,1)S(1)} %reshape.51), channel_id=1, source_target_pairs={{0,120},{8,0},{16,8},{24,16},{32,24},{40,32},{48,40},{56,48},{64,5... | collective-permute-start | bytes 3538952 | tf_op jit(solution)/shard_map/ppermute | solution.py:24
  169.7 55.9 %copy-start.5 = (bf16[288,2048]{1,0:T(8,128)(2,1)}, bf16[288,2048]{1,0:T(8,128)(2,1)S(1)}, u32[]{:S(2)}) copy-start(bf16[288,2048]{1,0:T(8,128)(2,1)S(1)} %collective-permute-done.1) | copy-start | bytes 3538948
  169.7 55.9 %collective-permute-start.2 = (bf16[288,2048]{1,0:T(8,128)(2,1)S(1)}, bf16[288,2048]{1,0:T(8,128)(2,1)S(1)}, u32[]{:S(2)}, u32[]{:S(2)}) collective-permute-start(bf16[288,2048]{1,0:T(8,128)(2,1)S(1)} %collective-permute-done.1), channel_id=1, source_target_pairs={{0,8},{8,16},{16,24},{24,32},{32,40},{40,48},{48,56},{56,64},{64,7... | collective-permute-start | bytes 3538952 | tf_op jit(solution)/shard_map/ppermute | solution.py:22
  169.7 4.8 %copy-start.3 = (bf16[288,2048]{1,0:T(8,128)(2,1)}, bf16[288,2048]{1,0:T(8,128)(2,1)S(1)}, u32[]{:S(2)}) copy-start(bf16[288,2048]{1,0:T(8,128)(2,1)S(1)} %collective-permute-done.8) | copy-start | bytes 3538948
  169.7 55.8 %collective-permute-start.9 = (bf16[288,2048]{1,0:T(8,128)(2,1)S(1)}, bf16[288,2048]{1,0:T(8,128)(2,1)S(1)}, u32[]{:S(2)}, u32[]{:S(2)}) collective-permute-start(bf16[288,2048]{1,0:T(8,128)(2,1)S(1)} %collective-permute-done.8), channel_id=1, source_target_pairs={{0,120},{8,0},{16,8},{24,16},{32,24},{40,32},{48,40},{56,48},{64,5... | collective-permute-start | bytes 3538952 | tf_op jit(solution)/shard_map/ppermute | solution.py:24
  225.5 27.9 %copy-start.9 = (bf16[288,2048]{1,0:T(8,128)(2,1)}, bf16[288,2048]{1,0:T(8,128)(2,1)S(1)}, u32[]{:S(2)}) copy-start(bf16[288,2048]{1,0:T(8,128)(2,1)S(1)} %collective-permute-done.2) | copy-start | bytes 3538948
  225.5 27.9 %collective-permute-start.3 = (bf16[288,2048]{1,0:T(8,128)(2,1)S(1)}, bf16[288,2048]{1,0:T(8,128)(2,1)S(1)}, u32[]{:S(2)}, u32[]{:S(2)}) collective-permute-start(bf16[288,2048]{1,0:T(8,128)(2,1)S(1)} %collective-permute-done.2), channel_id=1, source_target_pairs={{0,8},{8,16},{16,24},{24,32},{32,40},{40,48},{48,56},{56,64},{64,7... | collective-permute-start | bytes 3538952 | tf_op jit(solution)/shard_map/ppermute | solution.py:22
  225.6 4.8 %copy-start.7 = (bf16[288,2048]{1,0:T(8,128)(2,1)}, bf16[288,2048]{1,0:T(8,128)(2,1)S(1)}, u32[]{:S(2)}) copy-start(bf16[288,2048]{1,0:T(8,128)(2,1)S(1)} %collective-permute-done.9) | copy-start | bytes 3538948
  225.6 27.9 %collective-permute-start.10 = (bf16[288,2048]{1,0:T(8,128)(2,1)S(1)}, bf16[288,2048]{1,0:T(8,128)(2,1)S(1)}, u32[]{:S(2)}, u32[]{:S(2)}) collective-permute-start(bf16[288,2048]{1,0:T(8,128)(2,1)S(1)} %collective-permute-done.9), channel_id=1, source_target_pairs={{0,120},{8,0},{16,8},{24,16},{32,24},{40,32},{48,40},{56,48},{64,5... | collective-permute-start | bytes 3538952 | tf_op jit(solution)/shard_map/ppermute | solution.py:24
  253.4 53.7 %copy-start.15 = (bf16[288,2048]{1,0:T(8,128)(2,1)}, bf16[288,2048]{1,0:T(8,128)(2,1)S(1)}, u32[]{:S(2)}) copy-start(bf16[288,2048]{1,0:T(8,128)(2,1)S(1)} %collective-permute-done.3) | copy-start | bytes 3538948
  253.4 27.2 %collective-permute-start.4 = (bf16[288,2048]{1,0:T(8,128)(2,1)S(1)}, bf16[288,2048]{1,0:T(8,128)(2,1)}, u32[]{:S(2)}, u32[]{:S(2)}) collective-permute-start(bf16[288,2048]{1,0:T(8,128)(2,1)S(1)} %collective-permute-done.3), channel_id=1, source_target_pairs={{0,8},{8,16},{16,24},{24,32},{32,40},{40,48},{48,56},{56,64},{64,7... | collective-permute-start | bytes 3538952 | tf_op jit(solution)/shard_map/ppermute | solution.py:22
  253.5 4.8 %copy-start.11 = (bf16[288,2048]{1,0:T(8,128)(2,1)}, bf16[288,2048]{1,0:T(8,128)(2,1)S(1)}, u32[]{:S(2)}) copy-start(bf16[288,2048]{1,0:T(8,128)(2,1)S(1)} %collective-permute-done.10) | copy-start | bytes 3538948
  253.5 27.1 %collective-permute-start.11 = (bf16[288,2048]{1,0:T(8,128)(2,1)S(1)}, bf16[288,2048]{1,0:T(8,128)(2,1)S(1)}, u32[]{:S(2)}, u32[]{:S(2)}) collective-permute-start(bf16[288,2048]{1,0:T(8,128)(2,1)S(1)} %collective-permute-done.10), channel_id=1, source_target_pairs={{0,120},{8,0},{16,8},{24,16},{32,24},{40,32},{48,40},{56,48},{64,5... | collective-permute-start | bytes 3538952 | tf_op jit(solution)/shard_map/ppermute | solution.py:24
  280.6 26.5 %collective-permute-start.5 = (bf16[288,2048]{1,0:T(8,128)(2,1)}, bf16[288,2048]{1,0:T(8,128)(2,1)}, u32[]{:S(2)}, u32[]{:S(2)}) collective-permute-start(bf16[288,2048]{1,0:T(8,128)(2,1)} %collective-permute-done.4), channel_id=1, source_target_pairs={{0,8},{8,16},{16,24},{24,32},{32,40},{40,48},{48,56},{56,64},{64,7... | collective-permute-start | bytes 3538952 | tf_op jit(solution)/shard_map/ppermute | solution.py:22
  281.6 25.5 %collective-permute-start.12 = (bf16[288,2048]{1,0:T(8,128)(2,1)S(1)}, bf16[288,2048]{1,0:T(8,128)(2,1)}, u32[]{:S(2)}, u32[]{:S(2)}) collective-permute-start(bf16[288,2048]{1,0:T(8,128)(2,1)S(1)} %collective-permute-done.11), channel_id=1, source_target_pairs={{0,120},{8,0},{16,8},{24,16},{32,24},{40,32},{48,40},{56,48},{64,5... | collective-permute-start | bytes 3538952 | tf_op jit(solution)/shard_map/ppermute | solution.py:24
  307.1 25.6 %collective-permute-start.6 = (bf16[288,2048]{1,0:T(8,128)(2,1)}, bf16[288,2048]{1,0:T(8,128)(2,1)}, u32[]{:S(2)}, u32[]{:S(2)}) collective-permute-start(bf16[288,2048]{1,0:T(8,128)(2,1)} %collective-permute-done.5), channel_id=1, source_target_pairs={{0,8},{8,16},{16,24},{24,32},{32,40},{40,48},{48,56},{56,64},{64,7... | collective-permute-start | bytes 3538952 | tf_op jit(solution)/shard_map/ppermute | solution.py:22
  307.1 25.7 %collective-permute-start.13 = (bf16[288,2048]{1,0:T(8,128)(2,1)}, bf16[288,2048]{1,0:T(8,128)(2,1)}, u32[]{:S(2)}, u32[]{:S(2)}) collective-permute-start(bf16[288,2048]{1,0:T(8,128)(2,1)} %collective-permute-done.12), channel_id=1, source_target_pairs={{0,120},{8,0},{16,8},{24,16},{32,24},{40,32},{48,40},{56,48},{64,5... | collective-permute-start | bytes 3538952 | tf_op jit(solution)/shard_map/ppermute | solution.py:24
  332.7 24.8 %collective-permute-start.7 = (bf16[288,2048]{1,0:T(8,128)(2,1)}, bf16[288,2048]{1,0:T(8,128)(2,1)}, u32[]{:S(2)}, u32[]{:S(2)}) collective-permute-start(bf16[288,2048]{1,0:T(8,128)(2,1)} %collective-permute-done.6), channel_id=1, source_target_pairs={{0,8},{8,16},{16,24},{24,32},{32,40},{40,48},{48,56},{56,64},{64,7... | collective-permute-start | bytes 3538952 | tf_op jit(solution)/shard_map/ppermute | solution.py:22
  332.7 34.7 %copy-start.16 = (bf16[288,2048]{1,0:T(8,128)(2,1)S(1)}, bf16[288,2048]{1,0:T(8,128)(2,1)}, u32[]{:S(2)}) copy-start(bf16[288,2048]{1,0:T(8,128)(2,1)} %copy-done.15) | copy-start | bytes 3538948
  332.8 35.9 %copy-start.10 = (bf16[288,2048]{1,0:T(8,128)(2,1)S(1)}, bf16[288,2048]{1,0:T(8,128)(2,1)}, u32[]{:S(2)}) copy-start(bf16[288,2048]{1,0:T(8,128)(2,1)} %copy-done.9) | copy-start | bytes 3538948
  332.8 37.0 %copy-start.6 = (bf16[288,2048]{1,0:T(8,128)(2,1)S(1)}, bf16[288,2048]{1,0:T(8,128)(2,1)}, u32[]{:S(2)}) copy-start(bf16[288,2048]{1,0:T(8,128)(2,1)} %copy-done.5) | copy-start | bytes 3538948
  332.8 38.2 %copy-start.2 = (bf16[288,2048]{1,0:T(8,128)(2,1)S(1)}, bf16[288,2048]{1,0:T(8,128)(2,1)}, u32[]{:S(2)}) copy-start(bf16[288,2048]{1,0:T(8,128)(2,1)} %copy-done.1) | copy-start | bytes 3538948
  332.8 50.0 %collective-permute-start.14 = (bf16[288,2048]{1,0:T(8,128)(2,1)}, bf16[288,2048]{1,0:T(8,128)(2,1)S(1)}, u32[]{:S(2)}, u32[]{:S(2)}) collective-permute-start(bf16[288,2048]{1,0:T(8,128)(2,1)} %collective-permute-done.13), channel_id=1, source_target_pairs={{0,120},{8,0},{16,8},{24,16},{32,24},{40,32},{48,40},{56,48},{64,5... | collective-permute-start | bytes 3538952 | tf_op jit(solution)/shard_map/ppermute | solution.py:24
  362.4 10.9 %copy-start.4 = (bf16[288,2048]{1,0:T(8,128)(2,1)S(1)}, bf16[288,2048]{1,0:T(8,128)(2,1)}, u32[]{:S(2)}) copy-start(bf16[288,2048]{1,0:T(8,128)(2,1)} %copy-done.3) | copy-start | bytes 3538948
  364.9 9.5 %copy-start.8 = (bf16[288,2048]{1,0:T(8,128)(2,1)S(1)}, bf16[288,2048]{1,0:T(8,128)(2,1)}, u32[]{:S(2)}) copy-start(bf16[288,2048]{1,0:T(8,128)(2,1)} %copy-done.7) | copy-start | bytes 3538948
  367.5 8.2 %copy-start.12 = (bf16[288,2048]{1,0:T(8,128)(2,1)S(1)}, bf16[288,2048]{1,0:T(8,128)(2,1)}, u32[]{:S(2)}) copy-start(bf16[288,2048]{1,0:T(8,128)(2,1)} %copy-done.11) | copy-start | bytes 3538948
  368.6 8.2 %copy-start.14 = (bf16[288,2048]{1,0:T(8,128)(2,1)S(1)}, bf16[288,2048]{1,0:T(8,128)(2,1)}, u32[]{:S(2)}) copy-start(bf16[288,2048]{1,0:T(8,128)(2,1)} %copy-done.13) | copy-start | bytes 3538948
  (1 other events, 1.0 us)
Sparse Core Ops, SparseCore 0:
  41.6 188.7 all-gather.1
